TPU v7x, 32 devices: a whole 2x2x4 slice. The times are simulated.
32 devices in a mesh: row: 4 (over y, x), col: 8 (over z, core).
Axes of the slice: x: 2, y: 2, z: 4, core: 2. Of those that a mesh axis runs over, the one named last changes fastest.
Arguments:
- features: float32 [8, 1536, 256], P('col', 'row'), may hold values from -1000 to 1000
- tiles: bfloat16 [8, 4, 8, 9, 128, 128], P('col', 'row'), may hold values from -0.1875 to 0.1875
- tile_ids: int32 [8, 4, 8, 9], P('col', 'row'), may hold values from 0 to 35
- tile_counts: int32 [8, 4, 8], P('col', 'row'), may hold values from 1 to 9, as said below
Outputs:
- propagated: float32 [8, 1536, 256], P('col', 'row')
- residual_norms: float32 [3], replicated
Inputs may be any that keep to these rules, and one draw needn't show every extreme that they name: `tile_ids`: each id is a row tile times 3 plus a column tile; ids may repeat within a list. `tile_counts`: slots at or after the count hold values to be ignored; in every draw some device has 9 live slots for some source block.
All inputs are finite; a program needn't handle non-finite values.
Results may differ from a plain program's by a relative error of at most 0.014.
Values may be sent and summed in bfloat16 or wider, within the bound.
A program may use at most 64 MiB of HBM per device.

v0:
```python
import functools

import jax
import jax.numpy as jnp
from jax import lax
from jax.experimental import pallas as pl
from jax.experimental.pallas import tpu as pltpu
from jax.sharding import PartitionSpec as P

ITERS = 3
ALPHA = 0.1
CHUNKS = 2
PIECES = 2
MESH = pl.DeviceIdType.MESH


def kernel(
    nrow, ncol, ids_ref, counts_ref, feat_ref, tiles_ref, out_ref, norm_ref,
    table, lookup, dense, buf0, buf1, gathered, acc, current, stage, landed, squares, sq_row, sq_col,
    table_sem, tile_sem, ag_send, ag_recv, d2d_send, rs_send, rs_recv, sq_send_row, sq_recv_row, sq_send_col, sq_recv_col,
):
    nz = ncol // 2
    nodes, feats = feat_ref.shape
    slots = tiles_ref.shape[1]
    tile = tiles_ref.shape[-1]
    width = feats // CHUNKS
    row_tiles = nrow * nodes // tile
    col_tiles = nodes // tile
    places = row_tiles * col_tiles
    r = lax.axis_index("row")
    c = lax.axis_index("col")
    z = c // 2
    core = c % 2
    sibling = z * 2 + 1 - core
    bufs = (buf0, buf1)

    def tile_copy(q, slot):
        return pltpu.make_async_copy(
            tiles_ref.at[pl.ds(2 * q, 2)], bufs[slot].at[:, pl.ds(0, slots)], tile_sem.at[slot]
        )

    for slot in range(2):
        tile_copy(slot, slot).start()

    barrier = pltpu.get_barrier_semaphore()
    for k in range(1, ncol):
        pl.semaphore_signal(barrier, inc=1, device_id={"col": (c + k) % ncol}, device_id_type=MESH)
    for k in range(1, nrow):
        pl.semaphore_signal(barrier, inc=1, device_id={"row": (r + k) % nrow}, device_id_type=MESH)
    for ch in range(CHUNKS):
        cols = slice(ch * width, (ch + 1) * width)
        gathered[0, ch, c] = feat_ref[:, cols].astype(jnp.bfloat16)
    pl.semaphore_wait(barrier, ncol - 1 + nrow - 1)

    def peer(k):
        if nz == 4:
            return (z, z + 1 - 2 * (z % 2), (z + 2) % 4, 3 - z)[k]
        return (z + k) % nz

    piece = nodes // PIECES

    def block_copy(t, ch, source, target, send_sem, h):
        par = t % 2
        ref = gathered.at[par, ch, source, pl.ds(h * piece, piece)]
        return pltpu.make_async_remote_copy(
            src_ref=ref, dst_ref=ref, send_sem=send_sem, recv_sem=ag_recv.at[par, ch, source, h],
            device_id={"col": target}, device_id_type=MESH,
        )

    far = [nz == 4 and k == 3 for k in range(nz)]

    def direct(k, act):
        if far[k]:
            pl.when((z == 1) | (z == 2))(act)
        else:
            act()

    send_order = [2, 1, 3] if nz == 4 else list(range(1, nz))

    def gather_drain(ch, h):
        for k in send_order:
            def go(k=k):
                block_copy(0, ch, c, peer(k) * 2 + core, ag_send.at[ch, k, h], h).wait_send()
            direct(k, go)
        for k in range(nz):
            block_copy(0, ch, c, sibling, d2d_send.at[ch, k, h], h).wait_send()
        if nz == 4:
            @pl.when((z == 1) | (z == 2))
            def _():
                block_copy(0, ch, c, sibling, ag_send.at[ch, 0, h], h).wait_send()

    def gather_send(t, ch, h):
        if t > 0:
            gather_drain(ch, h)
        for k in send_order:
            def go(k=k):
                block_copy(t, ch, c, peer(k) * 2 + core, ag_send.at[ch, k, h], h).start()
            direct(k, go)
        block_copy(t, ch, c, sibling, d2d_send.at[ch, 0, h], h).start()

    def receive(t, ch, k):
        source = peer(k) * 2 + core
        for h in range(PIECES):
            block_copy(t, ch, source, sibling, d2d_send.at[ch, k, h], h).wait_recv()
            if nz == 4 and k == 2:
                @pl.when((z == 1) | (z == 2))
                def _():
                    block_copy(t, ch, source, 6 * (z - 1) + core, ag_send.at[ch, 0, h], h).start()
            block_copy(t, ch, source, sibling, d2d_send.at[ch, k, h], h).start()

    def share_copy(t, ch, k, h):
        par = t % 2
        span = pl.ds(h * piece, piece)
        return pltpu.make_async_remote_copy(
            src_ref=stage.at[ch, k - 1, span], dst_ref=landed.at[par, ch, r, span],
            send_sem=rs_send.at[ch, k - 1, h], recv_sem=rs_recv.at[par, ch, r, h],
            device_id={"row": (r + k) % nrow}, device_id_type=MESH,
        )

    def product(t, ch, k):
        q = peer(k)
        par = t % 2
        other = q * 2 + 1 - core
        for h in range(PIECES):
            block_copy(t, ch, other, sibling, d2d_send.at[ch, 0, h], h).wait_recv()
        source = gathered[par, ch, pl.ds(2 * q, 2)].reshape(2 * nodes, width)

        def part(rows):
            return jnp.dot(dense[q, rows], source, preferred_element_type=jnp.float32)

        if k < nz - 1:
            def one(j, carry):
                rows = pl.ds(j * nodes, nodes)
                acc[ch, rows] = part(rows) if k == 0 else acc[ch, rows] + part(rows)
                return carry
            lax.fori_loop(0, nrow, one, 0)
            return
        for h in range(PIECES):
            for k2 in range(1, nrow):
                rows = pl.ds((r + k2) % nrow * nodes + h * piece, piece)
                total = acc[ch, rows] + part(rows)
                if t > 0:
                    share_copy(t, ch, k2, h).wait_send()
                stage[ch, k2 - 1, h * piece : (h + 1) * piece] = total.astype(jnp.bfloat16)
                share_copy(t, ch, k2, h).start()
        rows = pl.ds(r * nodes, nodes)
        acc[ch, rows] = acc[ch, rows] + part(rows)

    def update(t, ch):
        par = t % 2
        cols = slice(ch * width, (ch + 1) * width)
        for h in range(PIECES):
            span = slice(h * piece, (h + 1) * piece)
            summed = acc[ch, pl.ds(r * nodes + h * piece, piece)]
            for k in range(1, nrow):
                j = (r + k) % nrow
                spot = landed.at[par, ch, j, pl.ds(h * piece, piece)]
                pltpu.make_async_remote_copy(
                    src_ref=spot, dst_ref=spot, send_sem=rs_send.at[ch, 0, h],
                    recv_sem=rs_recv.at[par, ch, j, h], device_id={"row": j}, device_id_type=MESH,
                ).wait_recv()
                summed = summed + landed[par, ch, j, span].astype(jnp.float32)
            teleport = feat_ref[span, cols]
            updated = (1.0 - ALPHA) * summed + ALPHA * teleport
            before = teleport if t == 0 else current[span, cols]
            if t < ITERS - 1:
                gathered[(t + 1) % 2, ch, c, span] = updated.astype(jnp.bfloat16)
                gather_send(t + 1, ch, h)
                current[span, cols] = updated
            else:
                out_ref[span, cols] = updated
            change = jnp.sum((updated - before) ** 2, axis=0, keepdims=True)
            squares[t : t + 1] = squares[t : t + 1] + change

    squares[...] = jnp.zeros_like(squares)
    for ch in range(CHUNKS):
        for h in range(PIECES):
            gather_send(0, ch, h)

    lane = lax.broadcasted_iota(jnp.int32, (1, table.shape[1]), 1)
    earlier = jnp.where(lane < places, slots, lane - places)

    def find(s, carry):
        ids = [ids_ref[s, k] for k in range(slots)]
        live = counts_ref[s]
        wanted = lane
        for k in range(slots):
            wanted = jnp.where(lane == places + k, ids[k], wanted)
        limit = jnp.minimum(earlier, live)
        found = jnp.full_like(lane, slots)
        for k in range(slots):
            found = jnp.where((wanted == ids[k]) & (limit > k), k, found)
        table[pl.ds(s, 1), :] = found
        return carry

    lax.fori_loop(0, ncol, find, 0)
    to_scalars = pltpu.make_async_copy(table, lookup, table_sem)
    to_scalars.start()
    zero = jnp.zeros((tile, tile), jnp.bfloat16)
    for slot in range(2):
        for half in range(2):
            bufs[slot][half, slots] = zero

    def build(step, carry):
        for slot in range(2):
            q = step * 2 + slot
            buf = bufs[slot]
            tile_copy(q, slot).wait()
            for half in range(2):
                s = 2 * q + half
                for k in range(1, slots):
                    buf[half, k] = buf[half, k] + buf[half, lookup[s, places + k]]
                for i in range(row_tiles):
                    for j in range(col_tiles):
                        at = half * nodes + j * tile
                        dense[q, i * tile : (i + 1) * tile, at : at + tile] = buf[half, lookup[s, i * col_tiles + j]]

            @pl.when(q + 2 < nz)
            def _():
                tile_copy(q + 2, slot).start()
        return carry

    to_scalars.wait()
    lax.fori_loop(0, nz // 2, build, 0)

    pending = None
    for t in range(ITERS):
        for ch in range(CHUNKS):
            for k in range(1, nz):
                if k == nz - 1 and pending is not None:
                    update(*pending)
                receive(t, ch, k)
                product(t, ch, k - 1)
            product(t, ch, nz - 1)
            pending = (t, ch)
    update(*pending)

    def sq_copy(axis, size, me, k, buffer, send, recv):
        return pltpu.make_async_remote_copy(
            src_ref=buffer.at[me], dst_ref=buffer.at[me], send_sem=send.at[k], recv_sem=recv.at[me],
            device_id={axis: (me + k) % size}, device_id_type=MESH,
        )

    total = squares[...]
    for axis, size, me, buffer, send, recv in (
        ("row", nrow, r, sq_row, sq_send_row, sq_recv_row),
        ("col", ncol, c, sq_col, sq_send_col, sq_recv_col),
    ):
        buffer[me] = total
        for k in range(1, size):
            sq_copy(axis, size, me, k, buffer, send, recv).start()
        for k in range(1, size):
            j = (me + k) % size
            pltpu.make_async_remote_copy(
                src_ref=buffer.at[me], dst_ref=buffer.at[j], send_sem=send.at[k], recv_sem=recv.at[j],
                device_id={axis: j}, device_id_type=MESH,
            ).wait_recv()
        total = buffer[0]
        for j in range(1, size):
            total = total + buffer[j]
        for k in range(1, size):
            sq_copy(axis, size, me, k, buffer, send, recv).wait_send()
    count = nrow * ncol * nodes * feats
    norms = jnp.sqrt(jnp.sum(total, axis=1, keepdims=True) / count)
    norm_ref[...] = jnp.broadcast_to(norms, norm_ref.shape)

    for ch in range(CHUNKS):
        for h in range(PIECES):
            gather_drain(ch, h)
            for k in range(1, nrow):
                share_copy(0, ch, k, h).wait_send()


def local(nrow, ncol, features, tiles, tile_ids, tile_counts):
    teleport = features[0]
    my_tiles = tiles[0, 0]
    my_ids = tile_ids[0, 0]
    my_counts = tile_counts[0, 0]
    nodes, feats = teleport.shape
    sources, slots, tile, _ = my_tiles.shape
    nz = ncol // 2
    width = feats // CHUNKS
    places = (nrow * nodes // tile) * (nodes // tile)
    lanes = pl.cdiv(places + slots, 128) * 128
    bf16, f32 = jnp.bfloat16, jnp.float32
    vmem, smem = pltpu.VMEM, pltpu.SMEM
    dma = pltpu.SemaphoreType.DMA
    out, norms = pl.pallas_call(
        functools.partial(kernel, nrow, ncol),
        out_shape=(jax.ShapeDtypeStruct((nodes, feats), f32), jax.ShapeDtypeStruct((8, 128), f32)),
        in_specs=[
            pl.BlockSpec(memory_space=smem), pl.BlockSpec(memory_space=smem),
            pl.BlockSpec(memory_space=vmem), pl.BlockSpec(memory_space=pl.ANY),
        ],
        out_specs=(pl.BlockSpec(memory_space=vmem), pl.BlockSpec(memory_space=vmem)),
        scratch_shapes=[
            vmem((ncol, lanes), jnp.int32),
            smem((ncol, lanes), jnp.int32),
            vmem((nz, nrow * nodes, 2 * nodes), bf16),
            vmem((2, slots + 1, tile, tile), bf16),
            vmem((2, slots + 1, tile, tile), bf16),
            vmem((2, CHUNKS, ncol, nodes, width), bf16),
            vmem((CHUNKS, nrow * nodes, width), f32),
            vmem((nodes, feats), f32),
            vmem((CHUNKS, nrow - 1, nodes, width), bf16),
            vmem((2, CHUNKS, nrow, nodes, width), bf16),
            vmem((8, width), f32),
            vmem((nrow, 8, width), f32),
            vmem((ncol, 8, width), f32),
            dma,
            dma((2,)),
            dma((CHUNKS, nz, PIECES)),
            dma((2, CHUNKS, ncol, PIECES)),
            dma((CHUNKS, nz, PIECES)),
            dma((CHUNKS, nrow - 1, PIECES)),
            dma((2, CHUNKS, nrow, PIECES)),
            dma((nrow,)),
            dma((nrow,)),
            dma((ncol,)),
            dma((ncol,)),
        ],
        compiler_params=pltpu.CompilerParams(collective_id=0, has_side_effects=True),
    )(my_ids, my_counts, teleport, my_tiles)
    return (out[None], norms[:ITERS, 0])


def solution(mesh):
    in_specs = (
        P("col", "row", None),
        P("col", "row", None, None, None, None),
        P("col", "row", None, None),
        P("col", "row", None),
    )
    out_specs = (P("col", "row", None), P())
    body = functools.partial(local, mesh.shape["row"], mesh.shape["col"])
    return jax.shard_map(body, mesh=mesh, in_specs=in_specs, out_specs=out_specs, check_vma=False)
```

profile of v0, /device:TPU:0, one launch (start us, length us, event | category | flops | bytes accessed | tf_op | source)
XLA Modules:
  0.0 84.9 jit_solution(9850330630997352222)
XLA Ops:
  0.6 81.2 %shard_map.59 = (f32[384,256]{1,0:T(8,128)}, f32[8,128]{1,0:T(8,128)}) custom-call(s32[8,9]{1,0:T(8,128)} %bitcast.8, s32[8]{0:T(128)} %bitcast.9, f32[384,256]{1,0:T(8,128)} %bitcast.6, bf16[8,9,128,128]{3,2,1,0:T(8,128)(2,1)} %bitcast.5), custom_call_target="tpu_custom_call" | custom-call | tf_op jit(solution)/shard_map/pallas_call | solution.py:288
  81.8 1.3 %slice_reduce_fusion = f32[3]{0:T(128)} fusion(f32[8,128]{1,0:T(8,128)} %get-tuple-element.5), kind=kLoop, calls=%fused_computation | loop fusion | bytes 24 | tf_op jit(solution)/shard_map/slice | solution.py:324
  83.1 1.8 %copy.7 = f32[1,384,256]{2,1,0:T(8,128)} copy(f32[1,384,256]{2,1,0:T(8,128)} %bitcast.7) | data formatting | bytes 786432
where the time goes:
time: 85.1 us; the launch traced here: 84.9 us
  Pallas kernels  81.2 us (95%)
  local copies, waits for them, and re-layouts  3.07 us (4%)
    pallas_call x1, Pallas kernels, local(): pl.pallas_call(functools.partial(kernel, nrow, ncol), out_shape=(jax.Shap...  81.2 us
    unnamed x1, local copies, waits for them, and re-layouts  1.77 us

commit v1 on v0

v1 whole, which is shorter than its diff:
```python
import functools

import jax
import jax.numpy as jnp
from jax import lax
from jax.experimental import pallas as pl
from jax.experimental.pallas import tpu as pltpu
from jax.sharding import PartitionSpec as P

ITERS = 3
ALPHA = 0.1
MESH = pl.DeviceIdType.MESH


def kernel(
    nrow, ncol, chunks, depth, ids_hbm, counts_hbm, feat_hbm, tiles_hbm, out_hbm, norm_ref,
    ids, counts, feat, teleport, table, lookup, dense, gathered, acc, current, stage, landed, squares, sums,
    small_sem, feat_sem, tile_sem, table_sem, out_sem, ag_send, ag_recv, d2d_send, rs_send, rs_recv, sq_send, sq_recv,
    *bufs,
):
    nz = ncol // 2
    nodes, feats = feat.shape
    slots = tiles_hbm.shape[1]
    tile = tiles_hbm.shape[-1]
    width = feats // chunks
    row_tiles = nrow * nodes // tile
    col_tiles = nodes // tile
    places = row_tiles * col_tiles
    steps = ITERS * chunks
    r = lax.axis_index("row")
    c = lax.axis_index("col")
    z = c // 2
    core = c % 2
    sibling = z * 2 + 1 - core
    middle = (z == 1) | (z == 2)

    def peer(k):
        if nz == 4:
            return (z, z + 1 - 2 * (z % 2), (z + 2) % 4, 3 - z)[k]
        return (z + k) % nz

    def tile_copy(k, slot):
        return pltpu.make_async_copy(
            tiles_hbm.at[pl.ds(2 * peer(k), 2)], bufs[slot].at[:, pl.ds(0, slots)], tile_sem.at[slot]
        )

    feat_copy = pltpu.make_async_copy(feat_hbm, feat, feat_sem)
    feat_copy.start()
    small_copies = (
        pltpu.make_async_copy(ids_hbm, ids, small_sem.at[0]),
        pltpu.make_async_copy(counts_hbm, counts, small_sem.at[1]),
    )
    for copy in small_copies:
        copy.start()
    for k in range(depth):
        tile_copy(k, k).start()

    barrier = pltpu.get_barrier_semaphore()
    for k in range(1, ncol):
        pl.semaphore_signal(barrier, inc=1, device_id={"col": (c + k) % ncol}, device_id_type=MESH)
    for k in range(1, nrow):
        pl.semaphore_signal(barrier, inc=1, device_id={"row": (r + k) % nrow}, device_id_type=MESH)

    def turn(j):
        lanes = slice(j * tile, (j + 1) * tile)
        teleport[lanes] = feat[:, lanes].T
        for ch in range(j * tile // width, (j + 1) * tile // width):
            gathered[0, ch, c] = teleport[ch * width : (ch + 1) * width].astype(jnp.bfloat16)

    feat_copy.wait()
    turn(0)
    pl.semaphore_wait(barrier, ncol - 1 + nrow - 1)

    def block_copy(n, source, target, send_sem):
        par, ch = n // chunks % 2, n % chunks
        ref = gathered.at[par, ch, source]
        return pltpu.make_async_remote_copy(
            src_ref=ref, dst_ref=ref, send_sem=send_sem, recv_sem=ag_recv.at[par, ch, source],
            device_id={"col": target}, device_id_type=MESH,
        )

    def direct(k, act):
        if nz == 4 and k == 3:
            pl.when(middle)(act)
        else:
            act()

    send_order = [2, 1, 3] if nz == 4 else list(range(1, nz))

    def gather_drain(ch):
        for k in send_order:
            def go(k=k):
                block_copy(ch, c, peer(k) * 2 + core, ag_send.at[ch, k]).wait_send()
            direct(k, go)
        for k in range(nz):
            block_copy(ch, c, sibling, d2d_send.at[ch, k]).wait_send()
        if nz == 4:
            @pl.when(middle)
            def _():
                block_copy(ch, c, sibling, ag_send.at[ch, 0]).wait_send()

    def send(n):
        ch = n % chunks
        if n >= chunks:
            gather_drain(ch)
        for k in send_order:
            def go(k=k):
                block_copy(n, c, peer(k) * 2 + core, ag_send.at[ch, k]).start()
            direct(k, go)
        block_copy(n, c, sibling, d2d_send.at[ch, 0]).start()

    def relay(n, k):
        ch = n % chunks
        source = peer(k) * 2 + core
        block_copy(n, source, sibling, d2d_send.at[ch, k]).wait_recv()
        if nz == 4 and k == 2:
            @pl.when(middle)
            def _():
                block_copy(n, source, 6 * (z - 1) + core, ag_send.at[ch, 0]).start()
        block_copy(n, source, sibling, d2d_send.at[ch, k]).start()

    def part(n, k):
        par, ch = n // chunks % 2, n % chunks
        q = peer(k)
        block_copy(n, q * 2 + 1 - core, sibling, d2d_send.at[ch, 0]).wait_recv()
        source = jnp.concatenate([gathered[par, ch, 2 * q], gathered[par, ch, 2 * q + 1]], axis=1)
        return jnp.dot(source, dense[k], preferred_element_type=jnp.float32)

    def product(n, k):
        ch = n % chunks
        got = part(n, k)
        for j in range(nrow):
            own = got[:, j * nodes : (j + 1) * nodes]
            acc[ch, j] = own if k == 0 else acc[ch, j] + own

    def share_copy(n, k):
        par, ch = n // chunks % 2, n % chunks
        j = r ^ k if nrow == 4 else (r + k) % nrow
        return pltpu.make_async_remote_copy(
            src_ref=stage.at[ch, j], dst_ref=landed.at[par, ch, r],
            send_sem=rs_send.at[ch, k], recv_sem=rs_recv.at[par, ch, r],
            device_id={"row": j}, device_id_type=MESH,
        )

    def finish(n):
        ch = n % chunks
        got = part(n, nz - 1)
        if n >= chunks:
            for k in range(1, nrow):
                share_copy(n, k).wait_send()
        for j in range(nrow):
            total = acc[ch, j] + got[:, j * nodes : (j + 1) * nodes]
            acc[ch, j] = total
            stage[ch, j] = total.astype(jnp.bfloat16)
        for k in range(nrow - 1, 0, -1):
            share_copy(n, k).start()

    def update(n):
        t, ch = n // chunks, n % chunks
        par = t % 2
        rows = slice(ch * width, (ch + 1) * width)
        summed = acc[ch, r]
        for k in range(1, nrow):
            j = r ^ k if nrow == 4 else (r + k) % nrow
            spot = landed.at[par, ch, j]
            pltpu.make_async_remote_copy(
                src_ref=spot, dst_ref=spot, send_sem=rs_send.at[ch, 0],
                recv_sem=rs_recv.at[par, ch, j], device_id={"row": j}, device_id_type=MESH,
            ).wait_recv()
            summed = summed + landed[par, ch, j].astype(jnp.float32)
        here = teleport[rows]
        updated = (1.0 - ALPHA) * summed + ALPHA * here
        before = here if t == 0 else current[rows]
        if t < ITERS - 1:
            gathered[(t + 1) % 2, ch, c] = updated.astype(jnp.bfloat16)
            send(n + chunks)
        current[rows] = updated
        change = (updated - before) ** 2
        change = jnp.sum(change.reshape(width // 8, 8, nodes), axis=0)
        total = change[:, :128]
        for j in range(1, nodes // 128):
            total = total + change[:, j * 128 : (j + 1) * 128]
        squares[t] = total if ch == 0 else squares[t] + total

    def emit(j):
        lanes = slice(j * tile, (j + 1) * tile)
        feat[:, lanes] = current[lanes].T
        copy = pltpu.make_async_copy(feat.at[:, lanes], out_hbm.at[:, lanes], out_sem.at[j])
        copy.start()
        return copy

    zero = jnp.zeros((tile, tile), jnp.bfloat16)
    lane = lax.broadcasted_iota(jnp.int32, (1, table.shape[1]), 1)
    earlier = jnp.where(lane < places, slots, lane - places)

    def find(s, carry):
        own = [ids[s, k] for k in range(slots)]
        live = counts[s]
        wanted = lane
        for k in range(slots):
            wanted = jnp.where(lane == places + k, own[k], wanted)
        limit = jnp.minimum(earlier, live)
        found = jnp.full_like(lane, slots)
        for k in range(slots):
            found = jnp.where((wanted == own[k]) & (limit > k), k, found)
        table[pl.ds(s, 1), :] = found
        return carry

    def build(k, slot):
        q = peer(k)
        buf = bufs[slot]
        tile_copy(k, slot).wait()
        for half in range(2):
            s = 2 * q + half
            for i in range(slots):
                buf[half, i] = buf[half, i].T
            for i in range(1, slots):
                buf[half, i] = buf[half, i] + buf[half, lookup[s, places + i]]
            for i in range(row_tiles):
                for j in range(col_tiles):
                    at = half * nodes + j * tile
                    dense[k, at : at + tile, i * tile : (i + 1) * tile] = buf[half, lookup[s, i * col_tiles + j]]

    send(0)
    if chunks > 1:
        send(1)
    for j in range(1, feats // tile):
        turn(j)
    for slot in range(depth):
        for half in range(2):
            bufs[slot][half, slots] = zero
    for copy in small_copies:
        copy.wait()
    lax.fori_loop(0, ncol, find, 0)
    to_scalars = pltpu.make_async_copy(table, lookup, table_sem)
    to_scalars.start()
    to_scalars.wait()
    if nz == depth:
        builds = [functools.partial(build, k, k) for k in range(nz)]
    else:
        def several(step, carry):
            for slot in range(depth):
                k = step * depth + slot
                build(k, slot)

                @pl.when(k + depth < nz)
                def _():
                    tile_copy(k + depth, slot).start()
            return carry

        lax.fori_loop(0, nz // depth, several, 0)
        builds = []

    def build_some(count):
        for _ in range(min(count, len(builds))):
            builds.pop(0)()

    build_some(2)
    copies = []

    def settle(n):
        update(n)
        done = (n % chunks + 1) * width
        if n // chunks == ITERS - 1 and done % tile == 0:
            copies.append(emit(done // tile - 1))

    if chunks >= 4:
        for m in range(1, steps + 4):
            if m >= 4:
                settle(m - 4)
            elif 1 < m < chunks:
                send(m)
            last, now = m - 2, m - 1
            if 0 <= last < steps:
                relay(last, nz - 1)
            if now < steps:
                for k in range(1, nz - 1):
                    relay(now, k)
                    build_some(1)
            build_some(4)
            if 0 <= last < steps:
                finish(last)
            if now < steps:
                for k in range(nz - 1):
                    product(now, k)
    else:
        build_some(4)
        for n in range(steps):
            for k in range(1, nz):
                if k == nz - 1 and n > 0:
                    settle(n - 1)
                relay(n, k)
                product(n, k - 1)
            finish(n)
        settle(steps - 1)

    size = nrow * ncol
    mine = r * ncol + c
    pad = jnp.zeros((8 - ITERS, 128), jnp.float32)
    sums[mine] = jnp.concatenate([jnp.sum(squares[t], axis=0, keepdims=True) for t in range(ITERS)] + [pad], axis=0)

    def sq_copy(dr, dc, slot):
        return pltpu.make_async_remote_copy(
            src_ref=sums.at[mine], dst_ref=sums.at[slot], send_sem=sq_send.at[dr, dc], recv_sem=sq_recv.at[slot],
            device_id={"row": (r + dr) % nrow, "col": (c + dc) % ncol}, device_id_type=MESH,
        )

    others = [(dr, dc) for dr in range(nrow) for dc in range(ncol) if dr or dc]
    for dr, dc in others:
        sq_copy(dr, dc, mine).start()
    for ch in range(chunks):
        gather_drain(ch)
        for k in range(1, nrow):
            share_copy(ch, k).wait_send()
    for copy in copies:
        copy.wait()
    for dr, dc in others:
        sq_copy(dr, dc, (r + dr) % nrow * ncol + (c + dc) % ncol).wait_recv()
    total = sums[0]
    for j in range(1, size):
        total = total + sums[j]
    count = size * nodes * feats
    norms = jnp.sqrt(jnp.sum(total, axis=1, keepdims=True) / count)
    norm_ref[...] = jnp.broadcast_to(norms, norm_ref.shape)
    for dr, dc in others:
        sq_copy(dr, dc, mine).wait_send()


def local(nrow, ncol, features, tiles, tile_ids, tile_counts):
    own = features[0]
    my_tiles = tiles[0, 0]
    my_ids = tile_ids[0, 0]
    my_counts = tile_counts[0, 0]
    nodes, feats = own.shape
    sources, slots, tile, _ = my_tiles.shape
    nz = ncol // 2
    chunks = 4 if nz == 4 else 2
    depth = 4 if nz == 4 else 2
    width = feats // chunks
    places = (nrow * nodes // tile) * (nodes // tile)
    lanes = pl.cdiv(places + slots, 128) * 128
    bf16, f32 = jnp.bfloat16, jnp.float32
    vmem, smem = pltpu.VMEM, pltpu.SMEM
    dma = pltpu.SemaphoreType.DMA
    anywhere = pl.BlockSpec(memory_space=pl.ANY)
    out, norms = pl.pallas_call(
        functools.partial(kernel, nrow, ncol, chunks, depth),
        out_shape=(jax.ShapeDtypeStruct((nodes, feats), f32), jax.ShapeDtypeStruct((8, 128), f32)),
        in_specs=[anywhere] * 4,
        out_specs=(anywhere, pl.BlockSpec(memory_space=vmem)),
        scratch_shapes=[
            smem((ncol, slots), jnp.int32),
            smem((ncol,), jnp.int32),
            vmem((nodes, feats), f32),
            vmem((feats, nodes), f32),
            vmem((ncol, lanes), jnp.int32),
            smem((ncol, lanes), jnp.int32),
            vmem((nz, 2 * nodes, nrow * nodes), bf16),
            vmem((2, chunks, ncol, width, nodes), bf16),
            vmem((chunks, nrow, width, nodes), f32),
            vmem((feats, nodes), f32),
            vmem((chunks, nrow, width, nodes), bf16),
            vmem((2, chunks, nrow, width, nodes), bf16),
            vmem((ITERS, 8, 128), f32),
            vmem((nrow * ncol, 8, 128), f32),
            dma((2,)),
            dma,
            dma((depth,)),
            dma,
            dma((feats // tile,)),
            dma((chunks, nz)),
            dma((2, chunks, ncol)),
            dma((chunks, nz)),
            dma((chunks, nrow)),
            dma((2, chunks, nrow)),
            dma((nrow, ncol)),
            dma((nrow * ncol,)),
        ]
        + [vmem((2, slots + 1, tile, tile), bf16)] * depth,
        compiler_params=pltpu.CompilerParams(collective_id=0, has_side_effects=True),
    )(my_ids, my_counts, own, my_tiles)
    return (out[None], norms[:ITERS, 0])


def solution(mesh):
    in_specs = (
        P("col", "row", None),
        P("col", "row", None, None, None, None),
        P("col", "row", None, None),
        P("col", "row", None),
    )
    out_specs = (P("col", "row", None), P())
    body = functools.partial(local, mesh.shape["row"], mesh.shape["col"])
    return jax.shard_map(body, mesh=mesh, in_specs=in_specs, out_specs=out_specs, check_vma=False)
```

time: 85.1 us -> 70.5 us (0.83)
  Pallas kernels: 81.2 us -> 66.5 us
    pallas_call x1, Pallas kernels: 81.2 us -> 66.5 us  [local(): pl.pallas_call(functools.partial(kernel, nrow, ncol, chunks, depth), out_...]
where the time goes in v1:
time: 70.5 us; the launch traced here: 70.3 us
  Pallas kernels  66.5 us (94%)
  local copies, waits for them, and re-layouts  3.07 us (4%)
    pallas_call x1, Pallas kernels, local(): pl.pallas_call(functools.partial(kernel, nrow, ncol, chunks, depth), out_...  66.5 us
    unnamed x1, local copies, waits for them, and re-layouts  1.77 us

profile of v1, /device:TPU:0, one launch (start us, length us, event | category | flops | bytes accessed | tf_op | source)
XLA Modules:
  0.0 70.3 jit_solution(9641223349380009545)
XLA Ops:
  0.6 66.5 %shard_map.59 = (f32[384,256]{1,0:T(8,128)}, f32[8,128]{1,0:T(8,128)}) custom-call(s32[8,9]{1,0:T(8,128)} %bitcast.8, s32[8]{0:T(128)} %bitcast.9, f32[384,256]{1,0:T(8,128)} %bitcast.6, bf16[8,9,128,128]{3,2,1,0:T(8,128)(2,1)} %bitcast.5), custom_call_target="tpu_custom_call" | custom-call | tf_op jit(solution)/shard_map/pallas_call | solution.py:346
  67.2 1.3 %slice_reduce_fusion = f32[3]{0:T(128)} fusion(f32[8,128]{1,0:T(8,128)} %get-tuple-element.5), kind=kLoop, calls=%fused_computation | loop fusion | bytes 24 | tf_op jit(solution)/shard_map/slice | solution.py:382
  68.5 1.8 %copy.7 = f32[1,384,256]{2,1,0:T(8,128)} copy(f32[1,384,256]{2,1,0:T(8,128)} %bitcast.7) | data formatting | bytes 786432

commit v2 on v1

v2 whole, which is shorter than its diff:
```python
import functools

import jax
import jax.numpy as jnp
from jax import lax
from jax.experimental import pallas as pl
from jax.experimental.pallas import tpu as pltpu
from jax.sharding import PartitionSpec as P

ITERS = 3
ALPHA = 0.1
MESH = pl.DeviceIdType.MESH


def kernel(
    nrow, ncol, chunks, depth, ids_hbm, counts_hbm, feat_hbm, tiles_hbm, current, norm_ref,
    ids, counts, feat, teleport, table, lookup, dense, gathered, acc, stage, landed, squares, sums,
    small_sem, feat_sem, tile_sem, table_sem, ag_send, ag_recv, d2d_recv, rs_send, rs_recv, sq_send, sq_recv,
    *bufs,
):
    nz = ncol // 2
    nodes, feats = feat.shape
    slots = tiles_hbm.shape[1]
    tile = tiles_hbm.shape[-1]
    width = feats // chunks
    row_tiles = nrow * nodes // tile
    col_tiles = nodes // tile
    places = row_tiles * col_tiles
    steps = ITERS * chunks
    r = lax.axis_index("row")
    c = lax.axis_index("col")
    z = c // 2
    core = c % 2
    sibling = z * 2 + 1 - core
    middle = (z == 1) | (z == 2)

    def peer(k):
        if nz == 4:
            return (z, z + 1 - 2 * (z % 2), (z + 2) % 4, 3 - z)[k]
        return (z + k) % nz

    def tile_copy(k, slot):
        return pltpu.make_async_copy(
            tiles_hbm.at[pl.ds(2 * peer(k), 2)], bufs[slot].at[:, pl.ds(0, slots)], tile_sem.at[slot]
        )

    feat_copy = pltpu.make_async_copy(feat_hbm, feat, feat_sem)
    feat_copy.start()
    small_copies = (
        pltpu.make_async_copy(ids_hbm, ids, small_sem.at[0]),
        pltpu.make_async_copy(counts_hbm, counts, small_sem.at[1]),
    )
    for copy in small_copies:
        copy.start()
    for k in range(depth):
        tile_copy(k, k).start()

    barrier = pltpu.get_barrier_semaphore()
    for k in range(1, ncol):
        pl.semaphore_signal(barrier, inc=1, device_id={"col": (c + k) % ncol}, device_id_type=MESH)
    for k in range(1, nrow):
        pl.semaphore_signal(barrier, inc=1, device_id={"row": (r + k) % nrow}, device_id_type=MESH)

    def turn(j):
        lanes = slice(j * tile, (j + 1) * tile)
        teleport[lanes] = feat[:, lanes].T
        for ch in range(j * tile // width, (j + 1) * tile // width):
            gathered[0, ch, c] = teleport[ch * width : (ch + 1) * width].astype(jnp.bfloat16)

    feat_copy.wait()
    turn(0)
    pl.semaphore_wait(barrier, ncol - 1 + nrow - 1)

    def block_copy(n, source, target, recv_sem, count=None):
        par, ch = n // chunks % 2, n % chunks
        ref = gathered.at[par, ch, source] if count is None else gathered.at[par, ch, pl.ds(0, count)]
        return pltpu.make_async_remote_copy(
            src_ref=ref, dst_ref=ref, send_sem=ag_send.at[ch], recv_sem=recv_sem,
            device_id={"col": target}, device_id_type=MESH,
        )

    def over(n, k):
        return ag_recv.at[n // chunks % 2, n % chunks, k - 1]

    def across(n, k):
        return d2d_recv.at[n // chunks % 2, n % chunks, k // (nz - 1)]

    def direct(k, act):
        if nz == 4 and k == 3:
            pl.when(middle)(act)
        else:
            act()

    send_order = [2, 1, 3] if nz == 4 else list(range(1, nz))

    def gather_drain(ch):
        if nz == 4:
            @pl.when(middle)
            def _():
                block_copy(ch, c, sibling, over(ch, 1), ncol).wait_send()

            @pl.when(jnp.logical_not(middle))
            def _():
                block_copy(ch, c, sibling, over(ch, 1), ncol - 2).wait_send()
        else:
            block_copy(ch, c, sibling, over(ch, 1), ncol - 1).wait_send()

    def send(n):
        if n >= chunks:
            gather_drain(n % chunks)
        for k in send_order:
            def go(k=k):
                block_copy(n, c, peer(k) * 2 + core, over(n, k if nz == 4 else nz - k)).start()
            direct(k, go)
        block_copy(n, c, sibling, across(n, 0)).start()

    def relay(n, k):
        source = peer(k) * 2 + core
        block_copy(n, source, sibling, over(n, k)).wait_recv()
        if nz == 4 and k == 2:
            @pl.when(middle)
            def _():
                block_copy(n, source, 6 * (z - 1) + core, over(n, 3)).start()
        block_copy(n, source, sibling, across(n, k)).start()

    def joined(n, last):
        if last:
            block_copy(n, c, sibling, across(n, nz - 1)).wait_recv()
        else:
            block_copy(n, c, sibling, across(n, 0), nz - 1).wait_recv()

    def part(n, k):
        par, ch = n // chunks % 2, n % chunks
        q = peer(k)
        source = jnp.concatenate([gathered[par, ch, 2 * q], gathered[par, ch, 2 * q + 1]], axis=1)
        return jnp.dot(source, dense[k], preferred_element_type=jnp.float32)

    def product(n, k):
        ch = n % chunks
        got = part(n, k)
        for j in range(nrow):
            own = got[:, j * nodes : (j + 1) * nodes]
            acc[ch, j] = own if k == 0 else acc[ch, j] + own

    def share_copy(n, k):
        par, ch = n // chunks % 2, n % chunks
        j = r ^ k if nrow == 4 else (r + k) % nrow
        return pltpu.make_async_remote_copy(
            src_ref=stage.at[ch, j], dst_ref=landed.at[par, ch, r],
            send_sem=rs_send.at[ch], recv_sem=rs_recv.at[par, ch],
            device_id={"row": j}, device_id_type=MESH,
        )

    def shares(n):
        par, ch = n // chunks % 2, n % chunks
        return pltpu.make_async_remote_copy(
            src_ref=stage.at[ch, pl.ds(0, nrow - 1)], dst_ref=landed.at[par, ch, pl.ds(0, nrow - 1)],
            send_sem=rs_send.at[ch], recv_sem=rs_recv.at[par, ch],
            device_id={"row": (r + 1) % nrow}, device_id_type=MESH,
        )

    def finish(n):
        ch = n % chunks
        joined(n, True)
        got = part(n, nz - 1)
        if n >= chunks:
            shares(n).wait_send()
        for j in range(nrow):
            total = acc[ch, j] + got[:, j * nodes : (j + 1) * nodes]
            acc[ch, j] = total
            stage[ch, j] = total.astype(jnp.bfloat16)
        for k in range(nrow - 1, 0, -1):
            share_copy(n, k).start()

    def update(n):
        t, ch = n // chunks, n % chunks
        par = t % 2
        rows = slice(ch * width, (ch + 1) * width)
        summed = acc[ch, r]
        shares(n).wait_recv()
        for k in range(1, nrow):
            j = r ^ k if nrow == 4 else (r + k) % nrow
            summed = summed + landed[par, ch, j].astype(jnp.float32)
        here = teleport[rows]
        updated = (1.0 - ALPHA) * summed + ALPHA * here
        before = here if t == 0 else current[rows]
        if t < ITERS - 1:
            gathered[(t + 1) % 2, ch, c] = updated.astype(jnp.bfloat16)
            send(n + chunks)
        current[rows] = updated
        change = (updated - before) ** 2
        change = jnp.sum(change.reshape(width // 8, 8, nodes), axis=0)
        total = change[:, :128]
        for j in range(1, nodes // 128):
            total = total + change[:, j * 128 : (j + 1) * 128]
        squares[t] = total if ch == 0 else squares[t] + total

    zero = jnp.zeros((tile, tile), jnp.bfloat16)
    lane = lax.broadcasted_iota(jnp.int32, (1, table.shape[1]), 1)
    earlier = jnp.where(lane < places, slots, lane - places)

    def find(s, carry):
        own = [ids[s, k] for k in range(slots)]
        live = counts[s]
        wanted = lane
        for k in range(slots):
            wanted = jnp.where(lane == places + k, own[k], wanted)
        limit = jnp.minimum(earlier, live)
        found = jnp.full_like(lane, slots)
        for k in range(slots):
            found = jnp.where((wanted == own[k]) & (limit > k), k, found)
        table[pl.ds(s, 1), :] = found
        return carry

    def flip(k, slot):
        buf = bufs[slot]
        tile_copy(k, slot).wait()
        for half in range(2):
            for i in range(slots):
                buf[half, i] = buf[half, i].T

    def build(k, slot):
        q = peer(k)
        buf = bufs[slot]
        for half in range(2):
            s = 2 * q + half
            for i in range(1, slots):
                buf[half, i] = buf[half, i] + buf[half, lookup[s, places + i]]
            for i in range(row_tiles):
                for j in range(col_tiles):
                    at = half * nodes + j * tile
                    dense[k, at : at + tile, i * tile : (i + 1) * tile] = buf[half, lookup[s, i * col_tiles + j]]

    send(0)
    if chunks > 1:
        send(1)
    for copy in small_copies:
        copy.wait()
    lax.fori_loop(0, ncol, find, 0)
    to_scalars = pltpu.make_async_copy(table, lookup, table_sem)
    to_scalars.start()
    for j in range(1, feats // tile):
        turn(j)
    for slot in range(depth):
        for half in range(2):
            bufs[slot][half, slots] = zero
    if nz == depth:
        for k in range(nz):
            flip(k, k)
        to_scalars.wait()
        for k in range(nz):
            build(k, k)
    else:
        def several(step, carry):
            for slot in range(depth):
                k = step * depth + slot
                flip(k, slot)
                build(k, slot)

                @pl.when(k + depth < nz)
                def _():
                    tile_copy(k + depth, slot).start()
            return carry

        to_scalars.wait()
        lax.fori_loop(0, nz // depth, several, 0)

    def settle(n):
        update(n)

    relay_order = [2, 1] if nz == 4 else list(range(1, nz - 1))
    if chunks >= 4:
        for m in range(1, steps + 3):
            last, now = m - 2, m - 1
            if 0 <= last < steps:
                relay(last, nz - 1)
            if now < steps:
                for k in relay_order:
                    relay(now, k)
            if 1 < m + 1 < chunks:
                send(m + 1)
            if 0 <= last < steps:
                finish(last)
            if now < steps:
                joined(now, False)
            for k in range(nz - 1):
                if k == nz - 3 and m >= 3:
                    settle(m - 3)
                if now < steps:
                    product(now, k)
    else:
        for n in range(steps):
            for k in range(1, nz):
                if k == nz - 1 and n > 0:
                    settle(n - 1)
                relay(n, k)
            joined(n, False)
            for k in range(nz - 1):
                product(n, k)
            finish(n)
        settle(steps - 1)

    size = nrow * ncol
    mine = r * ncol + c
    pad = jnp.zeros((8 - ITERS, 128), jnp.float32)
    sums[mine] = jnp.concatenate([jnp.sum(squares[t], axis=0, keepdims=True) for t in range(ITERS)] + [pad], axis=0)

    def sq_copy(j, q, slot, count=None):
        spot = sums.at[slot] if count is None else sums.at[pl.ds(0, count)]
        return pltpu.make_async_remote_copy(
            src_ref=spot, dst_ref=spot, send_sem=sq_send, recv_sem=sq_recv,
            device_id={"row": j, "col": q}, device_id_type=MESH,
        )

    for k in range(nz - 1, -1, -1):
        for side in range(1, -1, -1):
            for dr in range(nrow - 1, -1, -1):
                if k or side or dr:
                    j = r ^ dr if nrow == 4 else (r + dr) % nrow
                    sq_copy(j, peer(k) * 2 + (1 - core if side else core), mine).start()
    for ch in range(chunks):
        gather_drain(ch)
        shares(ch).wait_send()
    sq_copy(r, sibling, mine, size - 1).wait_recv()
    total = sums[0]
    for j in range(1, size):
        total = total + sums[j]
    count = size * nodes * feats
    norms = jnp.sqrt(jnp.sum(total, axis=1, keepdims=True) / count)
    norm_ref[...] = jnp.broadcast_to(norms, norm_ref.shape)
    sq_copy(r, sibling, mine, size - 1).wait_send()


def close(held_ref, norms_ref, out_ref, norm_ref):
    out_ref[0] = held_ref[...].T
    for t in range(ITERS):
        norm_ref[t] = norms_ref[t, 0]


def local(nrow, ncol, features, tiles, tile_ids, tile_counts):
    own = features[0]
    my_tiles = tiles[0, 0]
    my_ids = tile_ids[0, 0]
    my_counts = tile_counts[0, 0]
    nodes, feats = own.shape
    sources, slots, tile, _ = my_tiles.shape
    nz = ncol // 2
    chunks = 4 if nz == 4 else 2
    depth = 4 if nz == 4 else 2
    width = feats // chunks
    places = (nrow * nodes // tile) * (nodes // tile)
    lanes = pl.cdiv(places + slots, 128) * 128
    bf16, f32 = jnp.bfloat16, jnp.float32
    vmem, smem = pltpu.VMEM, pltpu.SMEM
    dma = pltpu.SemaphoreType.DMA
    anywhere = pl.BlockSpec(memory_space=pltpu.HBM)
    out, norms = pl.pallas_call(
        functools.partial(kernel, nrow, ncol, chunks, depth),
        out_shape=(jax.ShapeDtypeStruct((feats, nodes), f32), jax.ShapeDtypeStruct((8, 128), f32)),
        in_specs=[anywhere] * 4,
        out_specs=(pl.BlockSpec(memory_space=vmem), pl.BlockSpec(memory_space=vmem)),
        scratch_shapes=[
            smem((ncol, slots), jnp.int32),
            smem((ncol,), jnp.int32),
            vmem((nodes, feats), f32),
            vmem((feats, nodes), f32),
            vmem((ncol, lanes), jnp.int32),
            smem((ncol, lanes), jnp.int32),
            vmem((nz, 2 * nodes, nrow * nodes), bf16),
            vmem((2, chunks, ncol, width, nodes), bf16),
            vmem((chunks, nrow, width, nodes), f32),
            vmem((chunks, nrow, width, nodes), bf16),
            vmem((2, chunks, nrow, width, nodes), bf16),
            vmem((ITERS, 8, 128), f32),
            vmem((nrow * ncol, 8, 128), f32),
            dma((2,)),
            dma,
            dma((depth,)),
            dma,
            dma((chunks,)),
            dma((2, chunks, nz - 1)),
            dma((2, chunks, 2)),
            dma((chunks,)),
            dma((2, chunks)),
            dma,
            dma,
        ]
        + [vmem((2, slots + 1, tile, tile), bf16)] * depth,
        compiler_params=pltpu.CompilerParams(
            collective_id=0, has_side_effects=True, vmem_limit_bytes=(24 if nz == 4 else 60) * 2**20
        ),
    )(*(pltpu.with_memory_space_constraint(x, pltpu.HBM) for x in (my_ids, my_counts, own, my_tiles)))
    return tuple(
        pl.pallas_call(
            close,
            out_shape=(jax.ShapeDtypeStruct((1, nodes, feats), f32), jax.ShapeDtypeStruct((ITERS,), f32)),
            in_specs=[pl.BlockSpec(memory_space=vmem), pl.BlockSpec(memory_space=vmem)],
            out_specs=(pl.BlockSpec(memory_space=vmem), pl.BlockSpec(memory_space=smem)),
            compiler_params=pltpu.CompilerParams(vmem_limit_bytes=4 * 2**20),
        )(out, norms)
    )


def solution(mesh):
    in_specs = (
        P("col", "row", None),
        P("col", "row", None, None, None, None),
        P("col", "row", None, None),
        P("col", "row", None),
    )
    out_specs = (P("col", "row", None), P())
    body = functools.partial(local, mesh.shape["row"], mesh.shape["col"])
    return jax.shard_map(body, mesh=mesh, in_specs=in_specs, out_specs=out_specs, check_vma=False)
```

time: 70.5 us -> 64 us (0.908)
  Pallas kernels: 66.5 us -> 63.1 us
  local copies, waits for them, and re-layouts: 3.07 us -> 0 us
    pallas_call x1, Pallas kernels: 66.5 us -> 62.1 us  [local(): pl.pallas_call(functools.partial(kernel, nrow, ncol, chunks, depth), out_...]
    unnamed x1 -> x0, local copies, waits for them, and re-layouts: 1.77 us -> none
    slice x1 -> x0, local copies, waits for them, and re-layouts: 1.3 us -> none  [local(): return (out[None], norms[:ITERS, 0])]
    pallas_call x0 -> x1, Pallas kernels: none -> 0.93 us  [local(): pl.pallas_call(close, out_shape=(jax.ShapeDtypeStruct((1, nodes, feats),...]
where the time goes in v2:
time: 64 us; the launch traced here: 63.9 us
  Pallas kernels  63.1 us (99%)
  between operations  0.8 us (1%)
    pallas_call x1, Pallas kernels, local(): pl.pallas_call(functools.partial(kernel, nrow, ncol, chunks, depth), out_...  62.1 us

profile of v2, /device:TPU:0, one launch (start us, length us, event | category | flops | bytes accessed | tf_op | source)
XLA Modules:
  0.0 63.9 jit_solution(3544908053674600694)
XLA Ops:
  0.6 62.1 %shard_map.59 = (f32[256,384]{1,0:T(8,128)S(1)}, f32[8,128]{1,0:T(8,128)S(1)}) custom-call(s32[8,9]{1,0:T(8,128)} %bitcast.6, s32[8]{0:T(128)} %bitcast.7, f32[384,256]{1,0:T(8,128)} %bitcast.5, bf16[8,9,128,128]{3,2,1,0:T(8,128)(2,1)} %bitcast.4), custom_call_target="tpu_custom_call" | custom-call | tf_op jit(solution)/shard_map/pallas_call | solution.py:357
  62.8 0.9 %shard_map.60 = (f32[1,384,256]{2,1,0:T(8,128)}, f32[3]{0:T(128)}) custom-call(f32[256,384]{1,0:T(8,128)S(1)} %get-tuple-element.4.held_ref, f32[8,128]{1,0:T(8,128)S(1)} %get-tuple-element.5.norms_ref), custom_call_target="tpu_custom_call" | custom-call | tf_op jit(solution)/shard_map/pallas_call | solution.py:394
